TPU v7x, 8 devices: a whole 2x2x1 slice. The times are simulated.
8 devices in a mesh: dp: 1 (over z), c: 2 (over y), r: 4 (over x, core).
Axes of the slice: x: 2, y: 2, z: 1, core: 2. Of those that a mesh axis runs over, the one named last changes fastest.
Arguments:
- x: bfloat16 [4096, 2048], P(('dp', 'r'), 'c')
- w: bfloat16 [2048, 16384], P('r', 'c')
- dy: bfloat16 [4096, 16384], P(('dp', 'r'), 'c')
Outputs:
- output 1: bfloat16 [4096, 2048], P(('dp', 'r'), 'c')
- output 2: float32 [2048, 16384], P(('dp', 'r'), 'c')
All inputs are finite; a program needn't handle non-finite values.
Results may differ from a plain program's by a relative error of at most 0.001.
Values are sent between devices in bfloat16 or wider.
A program may use at most 1 GiB of HBM per device.

v0:
```python
import jax
import jax.numpy as jnp
from jax import lax
from jax.sharding import PartitionSpec as P


def solution(mesh):
    def local(x, w, dy):
        w_col = lax.all_gather(w, "r", axis=0, tiled=True)
        dx_part = lax.dot_general(dy, w_col, (((1,), (1,)), ((), ())),
                                  preferred_element_type=jnp.float32)
        dx = lax.psum_scatter(dx_part, "c", scatter_dimension=1, tiled=True).astype(jnp.bfloat16)
        x_row = lax.all_gather(x, "c", axis=1, tiled=True)
        dw_part = lax.dot_general(x_row, dy, (((0,), (0,)), ((), ())),
                                  preferred_element_type=jnp.float32)
        dw = lax.psum_scatter(dw_part, "r", scatter_dimension=0, tiled=True)
        return dx, dw

    act = P(("dp", "r"), "c")
    return jax.shard_map(local, mesh=mesh, in_specs=(act, P("r", "c"), act),
                         out_specs=(act, act), check_vma=False)
```

profile of v0, /device:TPU:0, one launch (start us, length us, event | category | flops | bytes accessed | tf_op | source)
XLA Modules:
  0.0 816.3 jit_solution(1236534640196960256)
XLA Ops:
  7.2 0.0 all-gather.3.cloned.1.call-start
  7.2 0.7 all-gather.3.cloned.1.call-update
  7.9 0.0 all-gather.5.cloned.1.call-start
  7.9 0.7 all-gather.5.cloned.1.call-update
  8.6 0.0 reduce-scatter.5.cloned.1.call-start
  8.7 203.0 %all-gather.3.cloned.1.call-done = bf16[2048,8192]{1,0:T(8,128)(2,1)} async-done(((bf16[512,8192]{1,0:T(8,128)(2,1)}), bf16[2048,8192]{1,0:T(8,128)(2,1)}) %all-gather.3.cloned.1.call-update) | async-done | bytes 33554448 | tf_op jit(solution)/shard_map/all_gather | solution.py:9
  211.7 43.4 %fusion = f32[1024,2048]{1,0:T(8,128)} fusion(bf16[1024,8192]{1,0:T(8,128)(2,1)} %param.5, bf16[2048,8192]{1,0:T(8,128)(2,1)} %all-gather.3.cloned.1.call-done), kind=kOutput, calls=%fused_computation | convolution fusion | flops 34359738368 | bytes 58720256 | tf_op jit(solution)/shard_map/dot_general | solution.py:10
  255.1 0.0 reduce-scatter.5.cloned.1.call-update
  255.2 0.2 reduce-scatter.7.cloned.1.call-start
  255.4 12.1 %all-gather.5.cloned.1.call-done = bf16[1024,2048]{1,0:T(8,128)(2,1)} async-done(((bf16[1024,1024]{1,0:T(8,128)(2,1)}), bf16[1024,2048]{1,0:T(8,128)(2,1)}) %all-gather.5.cloned.1.call-update) | async-done | bytes 4194320 | tf_op jit(solution)/shard_map/all_gather | solution.py:13
  267.4 45.2 %fusion.1 = f32[2048,8192]{1,0:T(8,128)} fusion(bf16[1024,2048]{1,0:T(8,128)(2,1)} %all-gather.5.cloned.1.call-done, bf16[1024,8192]{1,0:T(8,128)(2,1)} %param.5), kind=kOutput, calls=%fused_computation.1 | convolution fusion | flops 34359738368 | bytes 88080384 | tf_op jit(solution)/shard_map/dot_general | solution.py:14
  312.6 0.0 reduce-scatter.7.cloned.1.call-update
  312.6 53.6 %reduce-scatter.5.cloned.1.call-done = f32[1024,1024]{1,0:T(8,128)} async-done(((f32[1024,2048]{1,0:T(8,128)}), f32[1024,1024]{1,0:T(8,128)}) %reduce-scatter.5.cloned.1.call-update) | async-done | bytes 4194320 | tf_op jit(solution)/shard_map/reduce_scatter | solution.py:12
  366.2 3.8 convert_element_type.3
  370.0 439.7 %reduce-scatter.7.cloned.1.call-done = f32[512,8192]{1,0:T(8,128)} async-done(((f32[2048,8192]{1,0:T(8,128)}), f32[512,8192]{1,0:T(8,128)}) %reduce-scatter.7.cloned.1.call-update) | async-done | bytes 16777232
Async XLA Ops:
  7.2 204.6 %all-gather.3.cloned.1.call-start = ((), (), s32[]{:S(2)}) async-start(), calls=%async_computation.2 | async-start | bytes 41943040 | tf_op jit(solution)/shard_map/all_gather | solution.py:9
  7.9 259.5 %all-gather.5.cloned.1.call-start = ((), (), s32[]{:S(2)}) async-start(), calls=%async_computation.4 | async-start | bytes 6291456 | tf_op jit(solution)/shard_map/all_gather | solution.py:13
  8.6 357.5 %reduce-scatter.5.cloned.1.call-start = ((), (), s32[]{:S(2)}) async-start(), calls=%async_computation.3 | async-start | bytes 12582912 | tf_op jit(solution)/shard_map/reduce_scatter | solution.py:12
  255.2 554.6 %reduce-scatter.7.cloned.1.call-start = ((), (), s32[]{:S(2)}) async-start(), calls=%async_computation.5 | async-start | bytes 83886080
Sparse Core Ops, SparseCore 0:
  9.5 202.1 all-gather.2
  213.2 54.1 all-gather.4
  269.7 96.4 reduce-scatter.4
  369.2 440.5 reduce-scatter.6
where the time goes:
time: 816 us
  waiting for transfers between devices  710 us (87%)
  matrix products  88.6 us (11%)
  between operations  13.8 us (2%)
    unnamed x5, waiting for transfers between devices  441 us
    all_gather x1, waiting for transfers between devices, local(): w_col = lax.all_gather(w, 'r', axis=0, tiled=True)  203 us
    reduce_scatter x1, waiting for transfers between devices, local(): lax.psum_scatter(dx_part, 'c', scatter_dimension=1, tiled=True)  53.6 us
    dot_general x1, matrix products, local(): lax.dot_general(x_row, dy, (((0,), (0,)), ((), ())), preferred_element_ty...  45.2 us
    dot_general x1, matrix products, local(): lax.dot_general(dy, w_col, (((1,), (1,)), ((), ())), preferred_element_ty...  43.4 us
  transfers between devices with their start and end apart: 4, of which 4 were waited for; matrix products, arithmetic and copies ran while one was open for 11% of the time, Pallas kernels for 0%

commit v1 on v0

v1 whole, which is shorter than its diff:
```python
import jax
import jax.numpy as jnp
from jax import lax
from jax.experimental import pallas as pl
from jax.experimental.pallas import tpu as pltpu
from jax.sharding import PartitionSpec as P

MESH = pl.DeviceIdType.MESH
T = 64
TILE = 1024


def kernel(x, w, dy, dx, dw, far, far2, near, wv, xg, buf, xt, part, part_in, out,
           load_s, w_s, xl_s, xs_s, xr_s, xf_s, ys_s, yr_s, ns_s, nr_s, fs_s, fr_s,
           ps_s, pr_s, os_s, or_s, ol_s):
    rows, half = x.shape[0], x.shape[1] // 2
    cols = w.shape[1]
    steps = rows // T
    z, c, r = lax.axis_index("dp"), lax.axis_index("c"), lax.axis_index("r")
    chip, core = r // 2, r % 2
    far_chip = 1 - chip
    here = chip == c

    def device(cc, chip_, core_):
        return {"dp": z, "c": cc, "r": 2 * chip_ + core_}

    mate = device(c, chip, 1 - core)
    x_same, x_other = device(c, far_chip, core), device(c, far_chip, 1 - core)
    y_same, y_other = device(1 - c, chip, core), device(1 - c, chip, 1 - core)

    def remote(src, dst, send, recv, dev):
        return pltpu.make_async_remote_copy(src, dst, send, recv, device_id=dev,
                                            device_id_type=MESH)

    def x_block(t):
        return xg.at[pl.ds(pl.multiple_of(t * rows, rows), rows), :]

    def x_half(k):
        return x.at[:, pl.ds(pl.multiple_of(k * half, half), half)]

    def piece(ref, q):
        return ref.at[pl.ds(pl.multiple_of(q * T, T), T), :]

    barrier = pltpu.get_barrier_semaphore()
    peers = (mate, x_same, x_other, y_same, y_other)
    for p in peers:
        pl.semaphore_signal(barrier, inc=1, device_id=p, device_id_type=MESH)
    pl.semaphore_wait(barrier, len(peers))

    @pl.when(jnp.logical_not(here))
    def _():
        remote(x_half(core), x_block(r), xs_s.at[0], xr_s.at[r], x_same).start()
        remote(x_half(1 - core), x_block(r), xs_s.at[1], xr_s.at[r], x_other).start()

    @pl.when(here)
    def _():
        remote(x_half(core), x_block(r), xs_s.at[0], xr_s.at[r], y_same).start()
        remote(x_half(1 - core), x_block(r), xs_s.at[1], xr_s.at[r], y_other).start()
        remote(x_half(1 - core), x_block(r), xs_s.at[2], xr_s.at[r], mate).start()
        pltpu.make_async_copy(x_half(core), x_block(r), xl_s).start()

    @pl.loop(0, steps)
    def _(q):
        remote(piece(dy, q), piece(far, q), ys_s, yr_s.at[q], x_same).start()

    @pl.loop(0, steps)
    def _(q):
        remote(piece(dy, q), piece(near, q), ns_s, nr_s.at[q], mate).start()

    pltpu.make_async_copy(w, wv, w_s).start()

    @pl.loop(0, cols // TILE)
    def _(t):
        dw[:, pl.ds(pl.multiple_of(t * TILE, TILE), TILE)] = jnp.zeros((dw.shape[0], TILE), jnp.float32)

    pltpu.make_async_copy(w, wv, w_s).wait()

    mine, other = r, 2 * chip + 1 - core
    far_mine, far_other = 2 * far_chip + core, 2 * far_chip + 1 - core

    @pl.when(here)
    def _():
        pltpu.make_async_copy(x_half(core), x_block(r), xl_s).wait()

    @pl.when(jnp.logical_not(here))
    def _():
        remote(x_half(core), x_block(mine), xs_s.at[0], xr_s.at[mine], y_same).wait_recv()

    remote(x_half(core), x_block(other), xs_s.at[0], xr_s.at[other], y_same).wait_recv()

    def compute(slot, ta, tb, q):
        row = pl.multiple_of(q * T, T)
        xa = xg[pl.ds(pl.multiple_of(ta * rows + row, T), T), :]
        xb = xg[pl.ds(pl.multiple_of(tb * rows + row, T), T), :]
        xt[...] = jnp.concatenate([xa, xb], axis=0).T
        part[slot] = jnp.zeros(part.shape[1:], jnp.float32)

        @pl.loop(0, cols // TILE)
        def _(t):
            cs = pl.ds(pl.multiple_of(t * TILE, TILE), TILE)
            d = buf[:, cs]
            part[slot] += lax.dot_general(d, wv[:, cs], (((1,), (1,)), ((), ())),
                                          preferred_element_type=jnp.float32)
            dw[:, cs] += jnp.dot(xt[...], d, preferred_element_type=jnp.float32)

    def load(src, q, lo):
        return pltpu.make_async_copy(piece(src, q), buf.at[pl.ds(lo * T, T), :], load_s.at[lo])

    def send_part(slot):
        return remote(part.at[slot], part_in.at[slot], ps_s, pr_s.at[slot], y_same)

    @pl.loop(0, steps)
    def _(q):
        load(dy, q, 0).start()
        remote(piece(dy, q), piece(near, q), ns_s, nr_s.at[q], mate).wait_recv()
        load(near, q, 1).start()
        load(dy, q, 0).wait()
        load(near, q, 1).wait()
        compute(q, mine, other, q)

        @pl.when(jnp.logical_not(here))
        def _():
            send_part(q).start()

    for t in range(2):
        src_t = 2 * far_chip + t
        remote(x_half(core), x_block(src_t), xs_s.at[0], xr_s.at[src_t], x_same).wait_recv()

        @pl.when(here)
        def _():
            remote(x_block(src_t), x_block(src_t), xf_s.at[t], xr_s.at[src_t], y_same).start()

    def dx_piece(q):
        return dx.at[pl.ds(pl.multiple_of(q * T, T), T),
                     pl.ds(pl.multiple_of(core * half, half), half)]

    def finish(slot):
        send_part(slot).wait_recv()
        out[slot] = (part[slot] + part_in[slot]).astype(jnp.bfloat16)

    @pl.loop(0, steps)
    def _(q):
        slot = steps + q
        remote(piece(dy, q), piece(far, q), ys_s, yr_s.at[q], x_same).wait_recv()
        remote(piece(far, q), piece(far2, q), fs_s, fr_s.at[q], mate).start()
        load(far, q, 0).start()
        remote(piece(far, q), piece(far2, q), fs_s, fr_s.at[q], mate).wait_recv()
        load(far2, q, 1).start()
        load(far, q, 0).wait()
        load(far2, q, 1).wait()
        compute(slot, far_mine, far_other, q)

        @pl.when(jnp.logical_not(here))
        def _():
            send_part(slot).start()

        @pl.when(here)
        def _():
            finish(slot)
            remote(out.at[slot, pl.ds(0, T), :], dx_piece(q), os_s.at[0], or_s, x_same).start()
            remote(out.at[slot, pl.ds(T, T), :], dx_piece(q), os_s.at[1], or_s, x_other).start()
            finish(q)
            pltpu.make_async_copy(out.at[q, pl.ds(0, T), :], dx_piece(q), ol_s).start()
            remote(out.at[q, pl.ds(T, T), :], dx_piece(q), os_s.at[2], or_s, mate).start()

    remote(dy, far, ys_s, yr_s.at[0], x_same).wait_send()
    remote(dy, near, ns_s, nr_s.at[0], mate).wait_send()
    remote(far, far2, fs_s, fr_s.at[0], mate).wait_send()
    for t in range(2):
        remote(x_half(core), x_block(r), xs_s.at[t], xr_s.at[r], x_same).wait_send()

    @pl.when(jnp.logical_not(here))
    def _():
        remote(part, part_in, ps_s, pr_s.at[0], y_same).wait_send()
        remote(dx, dx, os_s.at[0], or_s, x_same).wait_recv()

    @pl.when(here)
    def _():
        remote(x_half(core), x_block(r), xs_s.at[2], xr_s.at[r], mate).wait_send()
        for t in range(2):
            remote(x_block(t), x_block(t), xf_s.at[t], xr_s.at[r], y_same).wait_send()
        dx_half = dx.at[:, pl.ds(0, half)]
        for t in range(3):
            remote(dx_half, dx_half, os_s.at[t], or_s, mate).wait_send()
        pltpu.make_async_copy(dx_half, dx_half, ol_s).wait()
        remote(dx_half, dx_half, os_s.at[0], or_s, mate).wait_recv()


def solution(mesh):
    def local(x, w, dy):
        rows, feats = x.shape
        half, cols = w.shape
        steps = rows // T
        any_ = pl.BlockSpec(memory_space=pl.ANY)
        dma = pltpu.SemaphoreType.DMA
        res = pl.pallas_call(
            kernel,
            out_shape=[
                jax.ShapeDtypeStruct((rows, feats), jnp.bfloat16),
                jax.ShapeDtypeStruct((half, cols), jnp.float32),
                jax.ShapeDtypeStruct((rows, cols), jnp.bfloat16),
                jax.ShapeDtypeStruct((rows, cols), jnp.bfloat16),
                jax.ShapeDtypeStruct((rows, cols), jnp.bfloat16),
            ],
            in_specs=[any_] * 3,
            out_specs=[any_, pl.BlockSpec(memory_space=pltpu.VMEM), any_, any_, any_],
            scratch_shapes=[
                pltpu.VMEM((half, cols), jnp.bfloat16),
                pltpu.VMEM((4 * rows, half), jnp.bfloat16),
                pltpu.VMEM((2 * T, cols), jnp.bfloat16),
                pltpu.VMEM((half, 2 * T), jnp.bfloat16),
                pltpu.VMEM((2 * steps, 2 * T, half), jnp.float32),
                pltpu.VMEM((2 * steps, 2 * T, half), jnp.float32),
                pltpu.VMEM((2 * steps, 2 * T, half), jnp.bfloat16),
                dma((2,)), dma, dma, dma((3,)), dma((4,)), dma((2,)),
                dma, dma((steps,)), dma, dma((steps,)), dma, dma((steps,)),
                dma, dma((2 * steps,)), dma((3,)), dma, dma,
            ],
            compiler_params=pltpu.CompilerParams(collective_id=0, has_side_effects=True,
                                                 vmem_limit_bytes=60 * 1024 * 1024),
        )(x, w, dy)
        return res[0], res[1]

    act = P(("dp", "r"), "c")
    return jax.shard_map(local, mesh=mesh, in_specs=(act, P("r", "c"), act),
                         out_specs=(act, act), check_vma=False)
```

time: 816 us -> 447 us (0.55)
  waiting for transfers between devices: 710 us -> 0 us
  Pallas kernels: 0 us -> 430 us
  matrix products: 88.6 us -> 0 us
  local copies, waits for them, and re-layouts: 0 us -> 14.7 us
  between operations: 13.8 us -> 0.64 us
    unnamed x5 -> x0, waiting for transfers between devices: 441 us -> none
    pallas_call x0 -> x1, Pallas kernels: none -> 430 us  [local(): pl.pallas_call(kernel, out_shape=[jax.ShapeDtypeStruct((rows, feats), jnp...]
    all_gather x2 -> x0, waiting for transfers between devices: 215 us -> none  [the longest x1 203 us: local(): w_col = lax.all_gather(w, 'r', axis=0, tiled=True)]
    dot_general x2 -> x0, matrix products: 88.6 us -> none  [the longest x1 45.2 us: local(): lax.dot_general(x_row, dy, (((0,), (0,)), ((), ())), preferred_element_ty...]
    reduce_scatter x1 -> x0, waiting for transfers between devices: 53.6 us -> none  [local(): lax.psum_scatter(dx_part, 'c', scatter_dimension=1, tiled=True)]
    unnamed x0 -> x2, local copies, waits for them, and re-layouts: none -> 14.7 us
  transfers between devices with their start and end apart: 4 -> 0, of which waited for: 4 -> 0; matrix products, arithmetic and copies ran while one was open for 11% -> 0% of each run, Pallas kernels for 0% -> 0%
where the time goes in v1:
time: 447 us; the launch traced here: 446 us
  Pallas kernels  430 us (96%)
  local copies, waits for them, and re-layouts  14.7 us (3%)
    pallas_call x1, Pallas kernels, local(): pl.pallas_call(kernel, out_shape=[jax.ShapeDtypeStruct((rows, feats), jnp...  430 us
    unnamed x2, local copies, waits for them, and re-layouts  14.7 us

profile of v1, /device:TPU:0, one launch (start us, length us, event | category | flops | bytes accessed | tf_op | source)
XLA Modules:
  0.0 445.7 jit_solution(3026531722593382961)
XLA Ops:
  0.6 430.4 %shard_map.50 = (bf16[1024,1024]{1,0:T(8,128)(2,1)}, f32[512,8192]{1,0:T(8,128)}, bf16[1024,8192]{1,0:T(8,128)(2,1)}, bf16[1024,8192]{1,0:T(8,128)(2,1)}, bf16[1024,8192]{1,0:T(8,128)(2,1)}) custom-call(bf16[1024,1024]{1,0:T(8,128)(2,1)} %x.1, bf16[512,8192]{1,0:T(8,128)(2,1)} %w.1, bf16[1024,8192]{1,0:T(8,128)(2,1)} %dy.1), custom_call_target="tpu_custom_call" | custom-call | tf_op jit(solution)/shard_map/pallas_call | solution.py:196
  431.0 3.1 copy.7
  434.1 11.7 %copy.8 = f32[512,8192]{1,0:T(8,128)} copy(f32[512,8192]{1,0:T(8,128)} %get-tuple-element.9) | data formatting | bytes 33554432

commit v2 on v1

--- a/solution.py
+++ b/solution.py
@@ -160,7 +160,7 @@
             remote(out.at[slot, pl.ds(0, T), :], dx_piece(q), os_s.at[0], or_s, x_same).start()
             remote(out.at[slot, pl.ds(T, T), :], dx_piece(q), os_s.at[1], or_s, x_other).start()
             finish(q)
-            pltpu.make_async_copy(out.at[q, pl.ds(0, T), :], dx_piece(q), ol_s).start()
+            dx[pl.ds(pl.multiple_of(q * T, T), T), pl.ds(pl.multiple_of(core * half, half), half)] = out[q, 0:T, :]
             remote(out.at[q, pl.ds(T, T), :], dx_piece(q), os_s.at[2], or_s, mate).start()
 
     remote(dy, far, ys_s, yr_s.at[0], x_same).wait_send()
@@ -182,8 +182,20 @@
         dx_half = dx.at[:, pl.ds(0, half)]
         for t in range(3):
             remote(dx_half, dx_half, os_s.at[t], or_s, mate).wait_send()
-        pltpu.make_async_copy(dx_half, dx_half, ol_s).wait()
         remote(dx_half, dx_half, os_s.at[0], or_s, mate).wait_recv()
+
+
+def store(dx_in, dw_in, dx, dw, sem):
+    n = 8
+    copies = [pltpu.make_async_copy(dx_in, dx, sem.at[n])]
+    step = dw.shape[0] // n
+    for i in range(n):
+        rs = pl.ds(i * step, step)
+        copies.append(pltpu.make_async_copy(dw_in.at[rs, :], dw.at[rs, :], sem.at[i]))
+    for cp in copies:
+        cp.start()
+    for cp in copies:
+        cp.wait()
 
 
 def solution(mesh):
@@ -196,14 +208,14 @@
         res = pl.pallas_call(
             kernel,
             out_shape=[
-                jax.ShapeDtypeStruct((rows, feats), jnp.bfloat16),
-                jax.ShapeDtypeStruct((half, cols), jnp.float32),
+                pltpu.VMEM((rows, feats), jnp.bfloat16),
+                pltpu.VMEM((half, cols), jnp.float32),
                 jax.ShapeDtypeStruct((rows, cols), jnp.bfloat16),
                 jax.ShapeDtypeStruct((rows, cols), jnp.bfloat16),
                 jax.ShapeDtypeStruct((rows, cols), jnp.bfloat16),
             ],
             in_specs=[any_] * 3,
-            out_specs=[any_, pl.BlockSpec(memory_space=pltpu.VMEM), any_, any_, any_],
+            out_specs=[pl.BlockSpec(memory_space=pltpu.VMEM), pl.BlockSpec(memory_space=pltpu.VMEM), any_, any_, any_],
             scratch_shapes=[
                 pltpu.VMEM((half, cols), jnp.bfloat16),
                 pltpu.VMEM((4 * rows, half), jnp.bfloat16),
@@ -217,9 +229,18 @@
                 dma, dma((2 * steps,)), dma((3,)), dma, dma,
             ],
             compiler_params=pltpu.CompilerParams(collective_id=0, has_side_effects=True,
-                                                 vmem_limit_bytes=60 * 1024 * 1024),
+                                                 vmem_limit_bytes=40 * 1024 * 1024),
         )(x, w, dy)
-        return res[0], res[1]
+        vmem = pl.BlockSpec(memory_space=pltpu.VMEM)
+        return pl.pallas_call(
+            store,
+            out_shape=[jax.ShapeDtypeStruct((rows, feats), jnp.bfloat16),
+                       jax.ShapeDtypeStruct((half, cols), jnp.float32)],
+            in_specs=[vmem, vmem],
+            out_specs=[any_, any_],
+            scratch_shapes=[dma((9,))],
+            compiler_params=pltpu.CompilerParams(vmem_limit_bytes=1024 * 1024),
+        )(res[0], res[1])
 
     act = P(("dp", "r"), "c")
     return jax.shard_map(local, mesh=mesh, in_specs=(act, P("r", "c"), act),

time: 447 us -> 433 us (0.969)
  local copies, waits for them, and re-layouts: 14.7 us -> 0 us
    unnamed x2 -> x0, local copies, waits for them, and re-layouts: 14.7 us -> none
    pallas_call x1 -> x2, Pallas kernels: 430 us -> 431 us  [the longest x1 424 us: local(): pl.pallas_call(kernel, out_shape=[pltpu.VMEM((rows, feats), jnp.bfloat16)...]
where the time goes in v2:
time: 433 us; the launch traced here: 431 us
  Pallas kernels  431 us (100%)
    pallas_call x1, Pallas kernels, local(): pl.pallas_call(kernel, out_shape=[pltpu.VMEM((rows, feats), jnp.bfloat16)...  424 us

profile of v2, /device:TPU:0, one launch (start us, length us, event | category | flops | bytes accessed | tf_op | source)
XLA Modules:
  0.0 431.4 jit_solution(1166467860979595438)
XLA Ops:
  0.6 424.2 %shard_map.50 = (bf16[1024,1024]{1,0:T(8,128)(2,1)S(1)}, f32[512,8192]{1,0:T(8,128)S(1)}, bf16[1024,8192]{1,0:T(8,128)(2,1)}, bf16[1024,8192]{1,0:T(8,128)(2,1)}, bf16[1024,8192]{1,0:T(8,128)(2,1)}) custom-call(bf16[1024,1024]{1,0:T(8,128)(2,1)} %x.1, bf16[512,8192]{1,0:T(8,128)(2,1)} %w.1, bf16[1024,8192]{1,0:T(8,128)(2,1)} %dy.1), custom_call_target="tpu_custom_call" | custom-call | tf_op jit(solution)/shard_map/pallas_call | solution.py:208
  424.8 6.6 %shard_map.51 = (bf16[1024,1024]{1,0:T(8,128)(2,1)}, f32[512,8192]{1,0:T(8,128)}) custom-call(bf16[1024,1024]{1,0:T(8,128)(2,1)S(1)} %get-tuple-element.4.dx_in, f32[512,8192]{1,0:T(8,128)S(1)} %get-tuple-element.5.dw_in), custom_call_target="tpu_custom_call" | custom-call | tf_op jit(solution)/shard_map/pallas_call | solution.py:235

commit v3 on v2

--- a/solution.py
+++ b/solution.py
@@ -8,14 +8,18 @@
 MESH = pl.DeviceIdType.MESH
 T = 64
 TILE = 1024
-
-
-def kernel(x, w, dy, dx, dw, far, far2, near, wv, xg, buf, xt, part, part_in, out,
+G = 32
+WIDE = 2048
+
+
+def kernel(x, w, dy, dx, dw, far, far2, near, wt, xg, buf, xt, last, part, part_in, out,
            load_s, w_s, xl_s, xs_s, xr_s, xf_s, ys_s, yr_s, ns_s, nr_s, fs_s, fr_s,
-           ps_s, pr_s, os_s, or_s, ol_s):
+           ts_s, tr_s, us_s, ur_s, ps_s, pr_s, os_s, or_s):
     rows, half = x.shape[0], x.shape[1] // 2
     cols = w.shape[1]
     steps = rows // T
+    main = steps - 1
+    wide = cols // WIDE
     z, c, r = lax.axis_index("dp"), lax.axis_index("c"), lax.axis_index("r")
     chip, core = r // 2, r % 2
     far_chip = 1 - chip
@@ -59,21 +63,44 @@
         remote(x_half(1 - core), x_block(r), xs_s.at[2], xr_s.at[r], mate).start()
         pltpu.make_async_copy(x_half(core), x_block(r), xl_s).start()
 
-    @pl.loop(0, steps)
+    @pl.loop(0, main)
     def _(q):
         remote(piece(dy, q), piece(far, q), ys_s, yr_s.at[q], x_same).start()
+
+    def wide_cols(p):
+        return pl.ds(pl.multiple_of(p * WIDE, WIDE), WIDE)
+
+    def send_last(g, p):
+        row = pl.multiple_of(main * T + g * G, G)
+        return remote(dy.at[pl.ds(row, G), wide_cols(p)], last.at[g, pl.ds(0, G), wide_cols(p)],
+                      ts_s, tr_s.at[g, p], x_same)
+
+    def pass_last(g, p):
+        return remote(last.at[g, pl.ds(0, G), wide_cols(p)], last.at[g, pl.ds(G, G), wide_cols(p)],
+                      us_s, ur_s.at[g, p], mate)
+
+    for g in range(2):
+        @pl.loop(0, wide)
+        def _(p):
+            send_last(g, p).start()
 
     @pl.loop(0, steps)
     def _(q):
         remote(piece(dy, q), piece(near, q), ns_s, nr_s.at[q], mate).start()
 
-    pltpu.make_async_copy(w, wv, w_s).start()
-
     @pl.loop(0, cols // TILE)
     def _(t):
         dw[:, pl.ds(pl.multiple_of(t * TILE, TILE), TILE)] = jnp.zeros((dw.shape[0], TILE), jnp.float32)
 
-    pltpu.make_async_copy(w, wv, w_s).wait()
+    for b in range(w.shape[0] // (2 * T)):
+        cp = pltpu.make_async_copy(w.at[pl.ds(b * 2 * T, 2 * T), :], buf, w_s)
+        cp.start()
+        cp.wait()
+
+        @pl.loop(0, cols // TILE)
+        def _(t):
+            cs = pl.ds(pl.multiple_of(t * TILE, TILE), TILE)
+            wt[cs, b * 2 * T:(b + 1) * 2 * T] = buf[:, cs].T
 
     mine, other = r, 2 * chip + 1 - core
     far_mine, far_other = 2 * far_chip + core, 2 * far_chip + 1 - core
@@ -99,8 +126,7 @@
         def _(t):
             cs = pl.ds(pl.multiple_of(t * TILE, TILE), TILE)
             d = buf[:, cs]
-            part[slot] += lax.dot_general(d, wv[:, cs], (((1,), (1,)), ((), ())),
-                                          preferred_element_type=jnp.float32)
+            part[slot] += jnp.dot(d, wt[cs, :], preferred_element_type=jnp.float32)
             dw[:, cs] += jnp.dot(xt[...], d, preferred_element_type=jnp.float32)
 
     def load(src, q, lo):
@@ -134,11 +160,14 @@
         return dx.at[pl.ds(pl.multiple_of(q * T, T), T),
                      pl.ds(pl.multiple_of(core * half, half), half)]
 
-    def finish(slot):
-        send_part(slot).wait_recv()
-        out[slot] = (part[slot] + part_in[slot]).astype(jnp.bfloat16)
-
-    @pl.loop(0, steps)
+    def finish_near(q):
+        send_part(q).wait_recv()
+        out[q] = (part[q] + part_in[q]).astype(jnp.bfloat16)
+        dx[pl.ds(pl.multiple_of(q * T, T), T),
+           pl.ds(pl.multiple_of(core * half, half), half)] = out[q, 0:T, :]
+        remote(out.at[q, pl.ds(T, T), :], dx_piece(q), os_s.at[2], or_s, mate).start()
+
+    @pl.loop(0, main)
     def _(q):
         slot = steps + q
         remote(piece(dy, q), piece(far, q), ys_s, yr_s.at[q], x_same).wait_recv()
@@ -156,16 +185,79 @@
 
         @pl.when(here)
         def _():
-            finish(slot)
+            send_part(slot).wait_recv()
+            out[slot] = (part[slot] + part_in[slot]).astype(jnp.bfloat16)
             remote(out.at[slot, pl.ds(0, T), :], dx_piece(q), os_s.at[0], or_s, x_same).start()
             remote(out.at[slot, pl.ds(T, T), :], dx_piece(q), os_s.at[1], or_s, x_other).start()
-            finish(q)
-            dx[pl.ds(pl.multiple_of(q * T, T), T), pl.ds(pl.multiple_of(core * half, half), half)] = out[q, 0:T, :]
-            remote(out.at[q, pl.ds(T, T), :], dx_piece(q), os_s.at[2], or_s, mate).start()
-
-    remote(dy, far, ys_s, yr_s.at[0], x_same).wait_send()
+            finish_near(q)
+
+    @pl.when(here)
+    def _():
+        finish_near(main)
+
+    slot = 2 * steps - 1
+    part[slot] = jnp.zeros(part.shape[1:], jnp.float32)
+    for g in range(2):
+        row = main * T + g * G
+        xa = xg[pl.ds(pl.multiple_of(far_mine * rows + row, G), G), :]
+        xb = xg[pl.ds(pl.multiple_of(far_other * rows + row, G), G), :]
+        xt[:, g * 2 * G:(g + 1) * 2 * G] = jnp.concatenate([xa, xb], axis=0).T
+
+    def arrive(g, p):
+        send_last(g, p).wait_recv()
+        pass_last(g, p).start()
+
+    def products(g, p):
+        pass_last(g, p).wait_recv()
+        cs = wide_cols(p)
+        part[slot, g * 2 * G:(g + 1) * 2 * G, :] += jnp.dot(
+            last[g, :, cs], wt[cs, :], preferred_element_type=jnp.float32)
+
+    def weights(g, p):
+        cs = wide_cols(p)
+        dw[:, cs] += jnp.dot(xt[:, g * 2 * G:(g + 1) * 2 * G], last[g, :, cs],
+                             preferred_element_type=jnp.float32)
+
+    arrive(0, 0)
+    for g in range(2):
+        row = main * T + g * G
+        group = pl.ds(g * 2 * G, 2 * G)
+
+        def send_group():
+            return remote(part.at[slot, group, :], part_in.at[slot, group, :], ps_s,
+                          pr_s.at[slot + g], y_same)
+
+        @pl.loop(0, wide - 1)
+        def _(p):
+            arrive(g, p + 1)
+            products(g, p)
+            weights(g, p)
+
+        if g == 0:
+            arrive(1, 0)
+        products(g, wide - 1)
+
+        @pl.when(jnp.logical_not(here))
+        def _():
+            send_group().start()
+
+        @pl.when(here)
+        def _():
+            send_group().wait_recv()
+            out[slot, group, :] = (part[slot, group, :] + part_in[slot, group, :]).astype(jnp.bfloat16)
+            target = dx.at[pl.ds(row, G), pl.ds(pl.multiple_of(core * half, half), half)]
+            for k, dev in ((0, x_same), (1, x_other)):
+                remote(out.at[slot, pl.ds(g * 2 * G + k * G, G), :], target, os_s.at[k], or_s, dev).start()
+
+        weights(g, wide - 1)
+
+    first = pl.ds(0, main * T)
+    remote(dy.at[first, :], far.at[first, :], ys_s, yr_s.at[0], x_same).wait_send()
+    rest = dy.at[pl.ds(main * T, 2 * G), :]
+    remote(rest, rest, ts_s, tr_s.at[0, 0], x_same).wait_send()
+    remote(rest, rest, us_s, ur_s.at[0, 0], mate).wait_send()
     remote(dy, near, ns_s, nr_s.at[0], mate).wait_send()
-    remote(far, far2, fs_s, fr_s.at[0], mate).wait_send()
+    remote(far.at[first, :], far2.at[first, :], fs_s, fr_s.at[0], mate).wait_send()
     for t in range(2):
         remote(x_half(core), x_block(r), xs_s.at[t], xr_s.at[r], x_same).wait_send()
 
@@ -217,19 +309,21 @@
             in_specs=[any_] * 3,
             out_specs=[pl.BlockSpec(memory_space=pltpu.VMEM), pl.BlockSpec(memory_space=pltpu.VMEM), any_, any_, any_],
             scratch_shapes=[
-                pltpu.VMEM((half, cols), jnp.bfloat16),
+                pltpu.VMEM((cols, half), jnp.bfloat16),
                 pltpu.VMEM((4 * rows, half), jnp.bfloat16),
                 pltpu.VMEM((2 * T, cols), jnp.bfloat16),
                 pltpu.VMEM((half, 2 * T), jnp.bfloat16),
+                pltpu.VMEM((2, 2 * G, cols), jnp.bfloat16),
                 pltpu.VMEM((2 * steps, 2 * T, half), jnp.float32),
                 pltpu.VMEM((2 * steps, 2 * T, half), jnp.float32),
                 pltpu.VMEM((2 * steps, 2 * T, half), jnp.bfloat16),
                 dma((2,)), dma, dma, dma((3,)), dma((4,)), dma((2,)),
                 dma, dma((steps,)), dma, dma((steps,)), dma, dma((steps,)),
-                dma, dma((2 * steps,)), dma((3,)), dma, dma,
+                dma, dma((2, cols // WIDE)), dma, dma((2, cols // WIDE)),
+                dma, dma((2 * steps + 1,)), dma((3,)), dma,
             ],
             compiler_params=pltpu.CompilerParams(collective_id=0, has_side_effects=True,
-                                                 vmem_limit_bytes=40 * 1024 * 1024),
+                                                 vmem_limit_bytes=44 * 1024 * 1024),
         )(x, w, dy)
         vmem = pl.BlockSpec(memory_space=pltpu.VMEM)
         return pl.pallas_call(

time: 433 us -> 424 us (0.979)
  Pallas kernels: 431 us -> 422 us
    pallas_call x1, Pallas kernels: 424 us -> 415 us  [local(): pl.pallas_call(kernel, out_shape=[pltpu.VMEM((rows, feats), jnp.bfloat16)...]
where the time goes in v3:
time: 424 us; the launch traced here: 422 us
  Pallas kernels  422 us (100%)
    pallas_call x1, Pallas kernels, local(): pl.pallas_call(kernel, out_shape=[pltpu.VMEM((rows, feats), jnp.bfloat16)...  415 us

profile of v3, /device:TPU:0, one launch (start us, length us, event | category | flops | bytes accessed | tf_op | source)
XLA Modules:
  0.0 422.2 jit_solution(8097158745601302036)
XLA Ops:
  0.6 415.0 %shard_map.50 = (bf16[1024,1024]{1,0:T(8,128)(2,1)S(1)}, f32[512,8192]{1,0:T(8,128)S(1)}, bf16[1024,8192]{1,0:T(8,128)(2,1)}, bf16[1024,8192]{1,0:T(8,128)(2,1)}, bf16[1024,8192]{1,0:T(8,128)(2,1)}) custom-call(bf16[1024,1024]{1,0:T(8,128)(2,1)} %x.1, bf16[512,8192]{1,0:T(8,128)(2,1)} %w.1, bf16[1024,8192]{1,0:T(8,128)(2,1)} %dy.1), custom_call_target="tpu_custom_call" | custom-call | tf_op jit(solution)/shard_map/pallas_call | solution.py:300
  415.7 6.6 %shard_map.51 = (bf16[1024,1024]{1,0:T(8,128)(2,1)}, f32[512,8192]{1,0:T(8,128)}) custom-call(bf16[1024,1024]{1,0:T(8,128)(2,1)S(1)} %get-tuple-element.4.dx_in, f32[512,8192]{1,0:T(8,128)S(1)} %get-tuple-element.5.dw_in), custom_call_target="tpu_custom_call" | custom-call | tf_op jit(solution)/shard_map/pallas_call | solution.py:329

commit v4 on v2

v4 whole, which is shorter than its diff:
```python
import jax
import jax.numpy as jnp
from jax import lax
from jax.experimental import pallas as pl
from jax.experimental.pallas import tpu as pltpu
from jax.sharding import PartitionSpec as P

MESH = pl.DeviceIdType.MESH
T = 64
TILE = 1024
AHEAD = 3


def kernel(x, w, dy, dx, dw, far, far2, near, wt, xg, relay, buf, xt, part, part_in, out,
           load_s, w_s, xl_s, xs_s, xr_s, lo_s, hi_s, rel_s, ys_s, yr_s, ns_s, nr_s, fs_s, fr_s,
           ps_s, pr_s, os_s, or_s):
    rows, half = x.shape[0], x.shape[1] // 2
    cols = w.shape[1]
    steps = rows // T
    hr = rows // 2
    z, c, r = lax.axis_index("dp"), lax.axis_index("c"), lax.axis_index("r")
    chip, core = r // 2, r % 2
    far_chip = 1 - chip
    here = chip == c
    there = jnp.logical_not(here)

    def device(cc, chip_, core_):
        return {"dp": z, "c": cc, "r": 2 * chip_ + core_}

    mate = device(c, chip, 1 - core)
    x_same, x_other = device(c, far_chip, core), device(c, far_chip, 1 - core)
    y_same, y_other = device(1 - c, chip, core), device(1 - c, chip, 1 - core)
    d_same, d_other = device(1 - c, far_chip, core), device(1 - c, far_chip, 1 - core)

    def remote(src, dst, send, recv, dev):
        return pltpu.make_async_remote_copy(src, dst, send, recv, device_id=dev,
                                            device_id_type=MESH)

    def x_rows(t, lo, n):
        return xg.at[pl.ds(pl.multiple_of(t * rows + lo, hr), n), :]

    def x_block(t):
        return x_rows(t, 0, rows)

    def x_part(k, lo, n):
        return x.at[pl.ds(lo, n), pl.ds(pl.multiple_of(k * half, half), half)]

    def piece(ref, q):
        return ref.at[pl.ds(pl.multiple_of(q * T, T), T), :]

    mine, other = r, 2 * chip + 1 - core
    far_mine, far_other = 2 * far_chip + core, 2 * far_chip + 1 - core

    barrier = pltpu.get_barrier_semaphore()
    peers = (mate, x_same, x_other, y_same, y_other, d_same, d_other)
    for p in peers:
        pl.semaphore_signal(barrier, inc=1, device_id=p, device_id_type=MESH)
    pl.semaphore_wait(barrier, len(peers))

    @pl.when(there)
    def _():
        remote(x_part(core, 0, hr), x_rows(r, 0, hr), xs_s.at[0], lo_s.at[core], x_same).start()
        remote(x_part(1 - core, 0, hr), x_rows(r, 0, hr), xs_s.at[1], lo_s.at[core], x_other).start()
        remote(x_part(core, hr, hr), relay.at[core], xs_s.at[2], rel_s.at[core], y_same).start()
        remote(x_part(1 - core, hr, hr), relay.at[core], xs_s.at[3], rel_s.at[core], y_other).start()

    def send_dy(q):
        return remote(piece(dy, q), piece(far, q), ys_s, yr_s.at[q], x_same)

    @pl.loop(0, AHEAD)
    def _(q):
        send_dy(q).start()

    @pl.when(there)
    def _():
        @pl.loop(AHEAD, steps)
        def _(q):
            send_dy(q).start()

    @pl.when(here)
    def _():
        remote(x_part(core, 0, rows), x_block(r), xs_s.at[0], xr_s.at[core], y_same).start()
        remote(x_part(1 - core, 0, rows), x_block(r), xs_s.at[1], xr_s.at[core], y_other).start()
        remote(x_part(1 - core, 0, rows), x_block(r), xs_s.at[2], xr_s.at[core], mate).start()
        pltpu.make_async_copy(x_part(core, 0, rows), x_block(r), xl_s).start()

    @pl.loop(0, steps)
    def _(q):
        remote(piece(dy, q), piece(near, q), ns_s, nr_s.at[q], mate).start()

    @pl.loop(0, cols // TILE)
    def _(t):
        dw[:, pl.ds(pl.multiple_of(t * TILE, TILE), TILE)] = jnp.zeros((dw.shape[0], TILE), jnp.float32)

    for b in range(w.shape[0] // (2 * T)):
        cp = pltpu.make_async_copy(w.at[pl.ds(b * 2 * T, 2 * T), :], buf, w_s)
        cp.start()
        cp.wait()

        @pl.loop(0, cols // TILE)
        def _(t):
            cs = pl.ds(pl.multiple_of(t * TILE, TILE), TILE)
            wt[cs, b * 2 * T:(b + 1) * 2 * T] = buf[:, cs].T

    @pl.when(here)
    def _():
        for t in range(2):
            remote(relay.at[t], relay.at[t], xs_s.at[5 + t], rel_s.at[t], y_same).wait_recv()
            remote(relay.at[t], x_rows(2 * chip + t, hr, hr), xs_s.at[5 + t], hi_s.at[t], x_same).start()

        @pl.loop(AHEAD, steps)
        def _(q):
            send_dy(q).start()

    @pl.when(here)
    def _():
        pltpu.make_async_copy(x_part(core, 0, rows), x_block(r), xl_s).wait()

    @pl.when(there)
    def _():
        remote(x_block(mine), x_block(mine), xs_s.at[0], xr_s.at[core], y_same).wait_recv()

    remote(x_block(other), x_block(other), xs_s.at[0], xr_s.at[1 - core], y_same).wait_recv()

    def compute(slot, ta, tb, q):
        row = pl.multiple_of(q * T, T)
        xa = xg[pl.ds(pl.multiple_of(ta * rows + row, T), T), :]
        xb = xg[pl.ds(pl.multiple_of(tb * rows + row, T), T), :]
        xt[...] = jnp.concatenate([xa, xb], axis=0).T
        part[slot] = jnp.zeros(part.shape[1:], jnp.float32)

        @pl.loop(0, cols // TILE)
        def _(t):
            cs = pl.ds(pl.multiple_of(t * TILE, TILE), TILE)
            d = buf[:, cs]
            part[slot] += jnp.dot(d, wt[cs, :], preferred_element_type=jnp.float32)
            dw[:, cs] += jnp.dot(xt[...], d, preferred_element_type=jnp.float32)

    def load(src, q, lo):
        return pltpu.make_async_copy(piece(src, q), buf.at[pl.ds(lo * T, T), :], load_s.at[lo])

    def send_part(slot):
        return remote(part.at[slot], part_in.at[slot], ps_s, pr_s.at[slot], y_same)

    @pl.loop(0, steps)
    def _(q):
        load(dy, q, 0).start()
        remote(piece(dy, q), piece(near, q), ns_s, nr_s.at[q], mate).wait_recv()
        load(near, q, 1).start()
        load(dy, q, 0).wait()
        load(near, q, 1).wait()
        compute(q, mine, other, q)

        @pl.when(there)
        def _():
            send_part(q).start()

    def pass_x(t, lo, recv, dev):
        rows_t = x_rows(2 * far_chip + t, lo, hr)
        return remote(rows_t, rows_t, xs_s.at[7 + t], recv.at[t], dev)

    for t in range(2):
        pass_x(t, 0, lo_s, x_same).wait_recv()

        @pl.when(here)
        def _():
            pass_x(t, 0, lo_s, y_same).start()

    for t in range(2):
        pass_x(t, hr, hi_s, x_same).wait_recv()

        @pl.when(there)
        def _():
            pass_x(t, hr, hi_s, y_same).start()

    def dx_piece(q):
        return dx.at[pl.ds(pl.multiple_of(q * T, T), T),
                     pl.ds(pl.multiple_of(core * half, half), half)]

    def add(slot):
        send_part(slot).wait_recv()
        out[slot] = (part[slot] + part_in[slot]).astype(jnp.bfloat16)

    def finish_far(q, dev_a, dev_b):
        slot = steps + q
        add(slot)
        remote(out.at[slot, pl.ds(0, T), :], dx_piece(q), os_s.at[0], or_s, dev_a).start()
        remote(out.at[slot, pl.ds(T, T), :], dx_piece(q), os_s.at[1], or_s, dev_b).start()

    def finish(q):
        @pl.when(jnp.logical_and(here, q % 2 == 1))
        def _():
            finish_far(q, x_same, x_other)

        @pl.when(jnp.logical_and(there, q % 2 == 0))
        def _():
            finish_far(q, d_same, d_other)

    @pl.loop(0, steps)
    def _(q):
        slot = steps + q
        send_dy(q).wait_recv()
        remote(piece(far, q), piece(far2, q), fs_s, fr_s.at[q], mate).start()
        load(far, q, 0).start()
        remote(piece(far, q), piece(far2, q), fs_s, fr_s.at[q], mate).wait_recv()
        load(far2, q, 1).start()
        load(far, q, 0).wait()
        load(far2, q, 1).wait()
        compute(slot, far_mine, far_other, q)

        @pl.when(jnp.logical_or(jnp.logical_and(there, q % 2 == 1), jnp.logical_and(here, q % 2 == 0)))
        def _():
            send_part(slot).start()

        @pl.when(q > 0)
        def _():
            finish(q - 1)

        @pl.when(here)
        def _():
            add(q)
            dx[pl.ds(pl.multiple_of(q * T, T), T),
               pl.ds(pl.multiple_of(core * half, half), half)] = out[q, 0:T, :]
            remote(out.at[q, pl.ds(T, T), :], dx_piece(q), os_s.at[2], or_s, mate).start()

    finish(steps - 1)

    remote(dy, far, ys_s, yr_s.at[0], x_same).wait_send()
    remote(dy, near, ns_s, nr_s.at[0], mate).wait_send()
    remote(far, far2, fs_s, fr_s.at[0], mate).wait_send()
    dx_half = dx.at[:, pl.ds(0, half)]
    dx_quarter = dx.at[pl.ds(0, hr), pl.ds(0, half)]
    for t in range(2):
        remote(dx_quarter, dx_quarter, os_s.at[t], or_s, x_same).wait_send()

    @pl.when(there)
    def _():
        for t in range(4):
            remote(x_part(0, 0, hr), x_rows(r, 0, hr), xs_s.at[t], lo_s.at[0], x_same).wait_send()
        for t in range(2):
            pass_x(t, hr, hi_s, y_same).wait_send()
        some = part.at[pl.ds(0, steps + steps // 2)]
        remote(some, some, ps_s, pr_s.at[0], y_same).wait_send()
        remote(dx, dx, os_s.at[0], or_s, x_same).wait_recv()

    @pl.when(here)
    def _():
        for t in range(3):
            remote(x_part(0, 0, rows), x_block(r), xs_s.at[t], xr_s.at[0], y_same).wait_send()
        for t in range(2):
            remote(relay.at[t], relay.at[t], xs_s.at[5 + t], rel_s.at[t], x_same).wait_send()
            pass_x(t, 0, lo_s, y_same).wait_send()
        some = part.at[pl.ds(0, steps // 2)]
        remote(some, some, ps_s, pr_s.at[0], y_same).wait_send()
        remote(dx_half, dx_half, os_s.at[2], or_s, mate).wait_send()
        remote(dx_half, dx_half, os_s.at[0], or_s, mate).wait_recv()


def store(dx_in, dw_in, dx, dw, sem):
    n = 8
    copies = [pltpu.make_async_copy(dx_in, dx, sem.at[n])]
    step = dw.shape[0] // n
    for i in range(n):
        rs = pl.ds(i * step, step)
        copies.append(pltpu.make_async_copy(dw_in.at[rs, :], dw.at[rs, :], sem.at[i]))
    for cp in copies:
        cp.start()
    for cp in copies:
        cp.wait()


def solution(mesh):
    def local(x, w, dy):
        rows, feats = x.shape
        half, cols = w.shape
        steps = rows // T
        any_ = pl.BlockSpec(memory_space=pl.ANY)
        vmem = pl.BlockSpec(memory_space=pltpu.VMEM)
        dma = pltpu.SemaphoreType.DMA
        res = pl.pallas_call(
            kernel,
            out_shape=[
                pltpu.VMEM((rows, feats), jnp.bfloat16),
                pltpu.VMEM((half, cols), jnp.float32),
                jax.ShapeDtypeStruct((rows, cols), jnp.bfloat16),
                jax.ShapeDtypeStruct((rows, cols), jnp.bfloat16),
                jax.ShapeDtypeStruct((rows, cols), jnp.bfloat16),
            ],
            in_specs=[any_] * 3,
            out_specs=[vmem, vmem, any_, any_, any_],
            scratch_shapes=[
                pltpu.VMEM((cols, half), jnp.bfloat16),
                pltpu.VMEM((4 * rows, half), jnp.bfloat16),
                pltpu.VMEM((2, rows // 2, half), jnp.bfloat16),
                pltpu.VMEM((2 * T, cols), jnp.bfloat16),
                pltpu.VMEM((half, 2 * T), jnp.bfloat16),
                pltpu.VMEM((2 * steps, 2 * T, half), jnp.float32),
                pltpu.VMEM((2 * steps, 2 * T, half), jnp.float32),
                pltpu.VMEM((2 * steps, 2 * T, half), jnp.bfloat16),
                dma((2,)), dma, dma, dma((9,)), dma((2,)), dma((2,)), dma((2,)), dma((2,)),
                dma, dma((steps,)), dma, dma((steps,)), dma, dma((steps,)),
                dma, dma((2 * steps,)), dma((3,)), dma,
            ],
            compiler_params=pltpu.CompilerParams(collective_id=0, has_side_effects=True,
                                                 vmem_limit_bytes=44 * 1024 * 1024),
        )(x, w, dy)
        return pl.pallas_call(
            store,
            out_shape=[jax.ShapeDtypeStruct((rows, feats), jnp.bfloat16),
                       jax.ShapeDtypeStruct((half, cols), jnp.float32)],
            in_specs=[vmem, vmem],
            out_specs=[any_, any_],
            scratch_shapes=[dma((9,))],
            compiler_params=pltpu.CompilerParams(vmem_limit_bytes=1024 * 1024),
        )(res[0], res[1])

    act = P(("dp", "r"), "c")
    return jax.shard_map(local, mesh=mesh, in_specs=(act, P("r", "c"), act),
                         out_specs=(act, act), check_vma=False)
```

time: 433 us -> 419 us (0.968)
  Pallas kernels: 431 us -> 417 us
    pallas_call x1, Pallas kernels: 424 us -> 410 us  [local(): pl.pallas_call(kernel, out_shape=[pltpu.VMEM((rows, feats), jnp.bfloat16)...]
where the time goes in v4:
time: 419 us; the launch traced here: 417 us
  Pallas kernels  417 us (100%)
    pallas_call x1, Pallas kernels, local(): pl.pallas_call(kernel, out_shape=[pltpu.VMEM((rows, feats), jnp.bfloat16)...  410 us

profile of v4, /device:TPU:0, one launch (start us, length us, event | category | flops | bytes accessed | tf_op | source)
XLA Modules:
  0.0 417.5 jit_solution(4945348333782647293)
XLA Ops:
  0.6 410.3 %shard_map.50 = (bf16[1024,1024]{1,0:T(8,128)(2,1)S(1)}, f32[512,8192]{1,0:T(8,128)S(1)}, bf16[1024,8192]{1,0:T(8,128)(2,1)}, bf16[1024,8192]{1,0:T(8,128)(2,1)}, bf16[1024,8192]{1,0:T(8,128)(2,1)}) custom-call(bf16[1024,1024]{1,0:T(8,128)(2,1)} %x.1, bf16[512,8192]{1,0:T(8,128)(2,1)} %w.1, bf16[1024,8192]{1,0:T(8,128)(2,1)} %dy.1), custom_call_target="tpu_custom_call" | custom-call | tf_op jit(solution)/shard_map/pallas_call | solution.py:280
  410.9 6.6 %shard_map.51 = (bf16[1024,1024]{1,0:T(8,128)(2,1)}, f32[512,8192]{1,0:T(8,128)}) custom-call(bf16[1024,1024]{1,0:T(8,128)(2,1)S(1)} %get-tuple-element.4.dx_in, f32[512,8192]{1,0:T(8,128)S(1)} %get-tuple-element.5.dw_in), custom_call_target="tpu_custom_call" | custom-call | tf_op jit(solution)/shard_map/pallas_call | solution.py:307

commit v5 on v4

--- a/solution.py
+++ b/solution.py
@@ -52,10 +52,19 @@
     far_mine, far_other = 2 * far_chip + core, 2 * far_chip + 1 - core
 
     barrier = pltpu.get_barrier_semaphore()
-    peers = (mate, x_same, x_other, y_same, y_other, d_same, d_other)
+    peers = (mate, x_same, x_other, y_same, y_other)
     for p in peers:
         pl.semaphore_signal(barrier, inc=1, device_id=p, device_id_type=MESH)
-    pl.semaphore_wait(barrier, len(peers))
+
+    @pl.when(there)
+    def _():
+        for p in (d_same, d_other):
+            pl.semaphore_signal(barrier, inc=1, device_id=p, device_id_type=MESH)
+        pl.semaphore_wait(barrier, len(peers) + 2)
+
+    @pl.when(here)
+    def _():
+        pl.semaphore_wait(barrier, len(peers))
 
     @pl.when(there)
     def _():
@@ -88,19 +97,27 @@
     def _(q):
         remote(piece(dy, q), piece(near, q), ns_s, nr_s.at[q], mate).start()
 
+    for b in range(2):
+        pltpu.make_async_copy(w.at[pl.ds(b * 2 * T, 2 * T), :], buf.at[b], w_s.at[b]).start()
+
     @pl.loop(0, cols // TILE)
     def _(t):
         dw[:, pl.ds(pl.multiple_of(t * TILE, TILE), TILE)] = jnp.zeros((dw.shape[0], TILE), jnp.float32)
 
-    for b in range(w.shape[0] // (2 * T)):
-        cp = pltpu.make_async_copy(w.at[pl.ds(b * 2 * T, 2 * T), :], buf, w_s)
-        cp.start()
-        cp.wait()
+    def load_w(b):
+        return pltpu.make_async_copy(w.at[pl.ds(b * 2 * T, 2 * T), :], buf.at[b % 2], w_s.at[b % 2])
+
+    blocks = w.shape[0] // (2 * T)
+    for b in range(blocks):
+        load_w(b).wait()
 
         @pl.loop(0, cols // TILE)
         def _(t):
             cs = pl.ds(pl.multiple_of(t * TILE, TILE), TILE)
-            wt[cs, b * 2 * T:(b + 1) * 2 * T] = buf[:, cs].T
+            wt[cs, b * 2 * T:(b + 1) * 2 * T] = buf[b % 2, :, cs].T
+
+        if b + 2 < blocks:
+            load_w(b + 2).start()
 
     @pl.when(here)
     def _():
@@ -132,21 +149,29 @@
         @pl.loop(0, cols // TILE)
         def _(t):
             cs = pl.ds(pl.multiple_of(t * TILE, TILE), TILE)
-            d = buf[:, cs]
+            d = buf[q % 2, :, cs]
             part[slot] += jnp.dot(d, wt[cs, :], preferred_element_type=jnp.float32)
             dw[:, cs] += jnp.dot(xt[...], d, preferred_element_type=jnp.float32)
 
     def load(src, q, lo):
-        return pltpu.make_async_copy(piece(src, q), buf.at[pl.ds(lo * T, T), :], load_s.at[lo])
+        return pltpu.make_async_copy(piece(src, q), buf.at[q % 2, pl.ds(lo * T, T), :], load_s.at[q % 2, lo])
 
     def send_part(slot):
         return remote(part.at[slot], part_in.at[slot], ps_s, pr_s.at[slot], y_same)
 
-    @pl.loop(0, steps)
-    def _(q):
+    def fetch_near(q):
         load(dy, q, 0).start()
         remote(piece(dy, q), piece(near, q), ns_s, nr_s.at[q], mate).wait_recv()
         load(near, q, 1).start()
+
+    fetch_near(0)
+
+    @pl.loop(0, steps)
+    def _(q):
+        @pl.when(q + 1 < steps)
+        def _():
+            fetch_near(q + 1)
+
         load(dy, q, 0).wait()
         load(near, q, 1).wait()
         compute(q, mine, other, q)
@@ -187,28 +212,25 @@
         remote(out.at[slot, pl.ds(0, T), :], dx_piece(q), os_s.at[0], or_s, dev_a).start()
         remote(out.at[slot, pl.ds(T, T), :], dx_piece(q), os_s.at[1], or_s, dev_b).start()
 
+    def by_o(q):
+        return jnp.logical_or(jnp.logical_and(q % 2 == 0, q < steps - 2), q == 1)
+
     def finish(q):
-        @pl.when(jnp.logical_and(here, q % 2 == 1))
+        @pl.when(jnp.logical_and(here, jnp.logical_not(by_o(q))))
         def _():
             finish_far(q, x_same, x_other)
 
-        @pl.when(jnp.logical_and(there, q % 2 == 0))
+        @pl.when(jnp.logical_and(there, by_o(q)))
         def _():
             finish_far(q, d_same, d_other)
 
-    @pl.loop(0, steps)
-    def _(q):
+    def work_far(q):
         slot = steps + q
-        send_dy(q).wait_recv()
-        remote(piece(far, q), piece(far2, q), fs_s, fr_s.at[q], mate).start()
-        load(far, q, 0).start()
-        remote(piece(far, q), piece(far2, q), fs_s, fr_s.at[q], mate).wait_recv()
-        load(far2, q, 1).start()
         load(far, q, 0).wait()
         load(far2, q, 1).wait()
         compute(slot, far_mine, far_other, q)
 
-        @pl.when(jnp.logical_or(jnp.logical_and(there, q % 2 == 1), jnp.logical_and(here, q % 2 == 0)))
+        @pl.when(there != by_o(q))
         def _():
             send_part(slot).start()
 
@@ -223,6 +245,19 @@
                pl.ds(pl.multiple_of(core * half, half), half)] = out[q, 0:T, :]
             remote(out.at[q, pl.ds(T, T), :], dx_piece(q), os_s.at[2], or_s, mate).start()
 
+    @pl.loop(0, steps)
+    def _(q):
+        send_dy(q).wait_recv()
+        load(far, q, 0).start()
+        remote(piece(far, q), piece(far2, q), fs_s, fr_s.at[q], mate).start()
+        remote(piece(far, q), piece(far2, q), fs_s, fr_s.at[q], mate).wait_recv()
+        load(far2, q, 1).start()
+
+        @pl.when(q > 0)
+        def _():
+            work_far(q - 1)
+
+    work_far(jnp.int32(steps - 1))
     finish(steps - 1)
 
     remote(dy, far, ys_s, yr_s.at[0], x_same).wait_send()
@@ -292,12 +327,12 @@
                 pltpu.VMEM((cols, half), jnp.bfloat16),
                 pltpu.VMEM((4 * rows, half), jnp.bfloat16),
                 pltpu.VMEM((2, rows // 2, half), jnp.bfloat16),
-                pltpu.VMEM((2 * T, cols), jnp.bfloat16),
+                pltpu.VMEM((2, 2 * T, cols), jnp.bfloat16),
                 pltpu.VMEM((half, 2 * T), jnp.bfloat16),
                 pltpu.VMEM((2 * steps, 2 * T, half), jnp.float32),
                 pltpu.VMEM((2 * steps, 2 * T, half), jnp.float32),
                 pltpu.VMEM((2 * steps, 2 * T, half), jnp.bfloat16),
-                dma((2,)), dma, dma, dma((9,)), dma((2,)), dma((2,)), dma((2,)), dma((2,)),
+                dma((2, 2)), dma((2,)), dma, dma((9,)), dma((2,)), dma((2,)), dma((2,)), dma((2,)),
                 dma, dma((steps,)), dma, dma((steps,)), dma, dma((steps,)),
                 dma, dma((2 * steps,)), dma((3,)), dma,
             ],

time: 419 us -> 419 us (level)
  no operation moved by 1% of the time
where the time goes in v5:
time: 419 us
  Pallas kernels  418 us (100%)
    pallas_call x1, Pallas kernels, local(): pl.pallas_call(kernel, out_shape=[pltpu.VMEM((rows, feats), jnp.bfloat16)...  412 us

profile of v5, /device:TPU:0, one launch (start us, length us, event | category | flops | bytes accessed | tf_op | source)
XLA Modules:
  0.0 418.9 jit_solution(520917225322913929)
XLA Ops:
  0.6 411.7 %shard_map.50 = (bf16[1024,1024]{1,0:T(8,128)(2,1)S(1)}, f32[512,8192]{1,0:T(8,128)S(1)}, bf16[1024,8192]{1,0:T(8,128)(2,1)}, bf16[1024,8192]{1,0:T(8,128)(2,1)}, bf16[1024,8192]{1,0:T(8,128)(2,1)}) custom-call(bf16[1024,1024]{1,0:T(8,128)(2,1)} %x.1, bf16[512,8192]{1,0:T(8,128)(2,1)} %w.1, bf16[1024,8192]{1,0:T(8,128)(2,1)} %dy.1), custom_call_target="tpu_custom_call" | custom-call | tf_op jit(solution)/shard_map/pallas_call | solution.py:315
  412.3 6.6 %shard_map.51 = (bf16[1024,1024]{1,0:T(8,128)(2,1)}, f32[512,8192]{1,0:T(8,128)}) custom-call(bf16[1024,1024]{1,0:T(8,128)(2,1)S(1)} %get-tuple-element.4.dx_in, f32[512,8192]{1,0:T(8,128)S(1)} %get-tuple-element.5.dw_in), custom_call_target="tpu_custom_call" | custom-call | tf_op jit(solution)/shard_map/pallas_call | solution.py:342

commit v6 on v5

--- a/solution.py
+++ b/solution.py
@@ -9,14 +9,16 @@
 T = 64
 TILE = 1024
 AHEAD = 3
+LAST = 2
 
 
 def kernel(x, w, dy, dx, dw, far, far2, near, wt, xg, relay, buf, xt, part, part_in, out,
            load_s, w_s, xl_s, xs_s, xr_s, lo_s, hi_s, rel_s, ys_s, yr_s, ns_s, nr_s, fs_s, fr_s,
-           ps_s, pr_s, os_s, or_s):
+           ts_s, tr_s, us_s, ur_s, ps_s, pr_s, os_s, or_s):
     rows, half = x.shape[0], x.shape[1] // 2
     cols = w.shape[1]
     steps = rows // T
+    main = steps - LAST
     hr = rows // 2
     z, c, r = lax.axis_index("dp"), lax.axis_index("c"), lax.axis_index("r")
     chip, core = r // 2, r % 2
@@ -76,15 +78,27 @@
     def send_dy(q):
         return remote(piece(dy, q), piece(far, q), ys_s, yr_s.at[q], x_same)
 
+    def send_last(g):
+        return remote(piece(dy, main + g), buf.at[2 + g, pl.ds(0, T), :], ts_s, tr_s.at[g], x_same)
+
+    def pass_last(g):
+        return remote(buf.at[2 + g, pl.ds(0, T), :], buf.at[2 + g, pl.ds(T, T), :], us_s, ur_s.at[g], mate)
+
+    def send_rest():
+        @pl.loop(AHEAD, main)
+        def _(q):
+            send_dy(q).start()
+
+        for g in range(LAST):
+            send_last(g).start()
+
     @pl.loop(0, AHEAD)
     def _(q):
         send_dy(q).start()
 
     @pl.when(there)
     def _():
-        @pl.loop(AHEAD, steps)
-        def _(q):
-            send_dy(q).start()
+        send_rest()
 
     @pl.when(here)
     def _():
@@ -125,9 +139,7 @@
             remote(relay.at[t], relay.at[t], xs_s.at[5 + t], rel_s.at[t], y_same).wait_recv()
             remote(relay.at[t], x_rows(2 * chip + t, hr, hr), xs_s.at[5 + t], hi_s.at[t], x_same).start()
 
-        @pl.loop(AHEAD, steps)
-        def _(q):
-            send_dy(q).start()
+        send_rest()
 
     @pl.when(here)
     def _():
@@ -139,7 +151,7 @@
 
     remote(x_block(other), x_block(other), xs_s.at[0], xr_s.at[1 - core], y_same).wait_recv()
 
-    def compute(slot, ta, tb, q):
+    def compute(slot, ta, tb, q, b):
         row = pl.multiple_of(q * T, T)
         xa = xg[pl.ds(pl.multiple_of(ta * rows + row, T), T), :]
         xb = xg[pl.ds(pl.multiple_of(tb * rows + row, T), T), :]
@@ -149,7 +161,7 @@
         @pl.loop(0, cols // TILE)
         def _(t):
             cs = pl.ds(pl.multiple_of(t * TILE, TILE), TILE)
-            d = buf[q % 2, :, cs]
+            d = buf[b, :, cs]
             part[slot] += jnp.dot(d, wt[cs, :], preferred_element_type=jnp.float32)
             dw[:, cs] += jnp.dot(xt[...], d, preferred_element_type=jnp.float32)
 
@@ -174,7 +186,7 @@
 
         load(dy, q, 0).wait()
         load(near, q, 1).wait()
-        compute(q, mine, other, q)
+        compute(q, mine, other, q, q % 2)
 
         @pl.when(there)
         def _():
@@ -213,7 +225,7 @@
         remote(out.at[slot, pl.ds(T, T), :], dx_piece(q), os_s.at[1], or_s, dev_b).start()
 
     def by_o(q):
-        return jnp.logical_or(jnp.logical_and(q % 2 == 0, q < steps - 2), q == 1)
+        return q % 2 == 0
 
     def finish(q):
         @pl.when(jnp.logical_and(here, jnp.logical_not(by_o(q))))
@@ -224,11 +236,9 @@
         def _():
             finish_far(q, d_same, d_other)
 
-    def work_far(q):
+    def work_far(q, b):
         slot = steps + q
-        load(far, q, 0).wait()
-        load(far2, q, 1).wait()
-        compute(slot, far_mine, far_other, q)
+        compute(slot, far_mine, far_other, q, b)
 
         @pl.when(there != by_o(q))
         def _():
@@ -245,7 +255,12 @@
                pl.ds(pl.multiple_of(core * half, half), half)] = out[q, 0:T, :]
             remote(out.at[q, pl.ds(T, T), :], dx_piece(q), os_s.at[2], or_s, mate).start()
 
-    @pl.loop(0, steps)
+    def work_loaded(q):
+        load(far, q, 0).wait()
+        load(far2, q, 1).wait()
+        work_far(q, q % 2)
+
+    @pl.loop(0, main)
     def _(q):
         send_dy(q).wait_recv()
         load(far, q, 0).start()
@@ -255,14 +270,24 @@
 
         @pl.when(q > 0)
         def _():
-            work_far(q - 1)
-
-    work_far(jnp.int32(steps - 1))
-    finish(steps - 1)
-
-    remote(dy, far, ys_s, yr_s.at[0], x_same).wait_send()
+            work_loaded(q - 1)
+
+    work_loaded(jnp.int32(main - 1))
+    for g in range(LAST):
+        send_last(g).wait_recv()
+        pass_last(g).start()
+        pass_last(g).wait_recv()
+        work_far(jnp.int32(main + g), 2 + g)
+
+    finish(jnp.int32(steps - 1))
+
+    first = pl.ds(0, main * T)
+    rest = dy.at[pl.ds(main * T, LAST * T), :]
+    remote(dy.at[first, :], far.at[first, :], ys_s, yr_s.at[0], x_same).wait_send()
+    remote(rest, rest, ts_s, tr_s.at[0], x_same).wait_send()
+    remote(rest, rest, us_s, ur_s.at[0], mate).wait_send()
     remote(dy, near, ns_s, nr_s.at[0], mate).wait_send()
-    remote(far, far2, fs_s, fr_s.at[0], mate).wait_send()
+    remote(far.at[first, :], far2.at[first, :], fs_s, fr_s.at[0], mate).wait_send()
     dx_half = dx.at[:, pl.ds(0, half)]
     dx_quarter = dx.at[pl.ds(0, hr), pl.ds(0, half)]
     for t in range(2):
@@ -327,13 +352,14 @@
                 pltpu.VMEM((cols, half), jnp.bfloat16),
                 pltpu.VMEM((4 * rows, half), jnp.bfloat16),
                 pltpu.VMEM((2, rows // 2, half), jnp.bfloat16),
-                pltpu.VMEM((2, 2 * T, cols), jnp.bfloat16),
+                pltpu.VMEM((2 + LAST, 2 * T, cols), jnp.bfloat16),
                 pltpu.VMEM((half, 2 * T), jnp.bfloat16),
                 pltpu.VMEM((2 * steps, 2 * T, half), jnp.float32),
                 pltpu.VMEM((2 * steps, 2 * T, half), jnp.float32),
                 pltpu.VMEM((2 * steps, 2 * T, half), jnp.bfloat16),
                 dma((2, 2)), dma((2,)), dma, dma((9,)), dma((2,)), dma((2,)), dma((2,)), dma((2,)),
                 dma, dma((steps,)), dma, dma((steps,)), dma, dma((steps,)),
+                dma, dma((LAST,)), dma, dma((LAST,)),
                 dma, dma((2 * steps,)), dma((3,)), dma,
             ],
             compiler_params=pltpu.CompilerParams(collective_id=0, has_side_effects=True,

time: 419 us -> 417 us (level)
  no operation moved by 1% of the time
where the time goes in v6:
time: 417 us
  Pallas kernels  416 us (100%)
    pallas_call x1, Pallas kernels, local(): pl.pallas_call(kernel, out_shape=[pltpu.VMEM((rows, feats), jnp.bfloat16)...  409 us

profile of v6, /device:TPU:0, one launch (start us, length us, event | category | flops | bytes accessed | tf_op | source)
XLA Modules:
  0.0 416.6 jit_solution(14349117364437907471)
XLA Ops:
  0.6 409.4 %shard_map.50 = (bf16[1024,1024]{1,0:T(8,128)(2,1)S(1)}, f32[512,8192]{1,0:T(8,128)S(1)}, bf16[1024,8192]{1,0:T(8,128)(2,1)}, bf16[1024,8192]{1,0:T(8,128)(2,1)}, bf16[1024,8192]{1,0:T(8,128)(2,1)}) custom-call(bf16[1024,1024]{1,0:T(8,128)(2,1)} %x.1, bf16[512,8192]{1,0:T(8,128)(2,1)} %w.1, bf16[1024,8192]{1,0:T(8,128)(2,1)} %dy.1), custom_call_target="tpu_custom_call" | custom-call | tf_op jit(solution)/shard_map/pallas_call | solution.py:340
  410.1 6.6 %shard_map.51 = (bf16[1024,1024]{1,0:T(8,128)(2,1)}, f32[512,8192]{1,0:T(8,128)}) custom-call(bf16[1024,1024]{1,0:T(8,128)(2,1)S(1)} %get-tuple-element.4.dx_in, f32[512,8192]{1,0:T(8,128)S(1)} %get-tuple-element.5.dw_in), custom_call_target="tpu_custom_call" | custom-call | tf_op jit(solution)/shard_map/pallas_call | solution.py:368
